TPU v7x, 8 devices: a whole 2x2x1 slice. The times are simulated.
8 devices in a mesh: fsdp: 8 (over z, y, x, core).
Axes of the slice: x: 2, y: 2, z: 1, core: 2. Of those that a mesh axis runs over, the one named last changes fastest.
Arguments:
- grad_mat: bfloat16 [8, 29491200], P('fsdp')
- grad_vec: bfloat16 [8, 11264], P('fsdp')
- master_mat: float32 [29491200], P('fsdp')
- moment_mat: float32 [29491200], P('fsdp')
- second_mat: float32 [29491200], P('fsdp')
- master_vec: float32 [11264], P('fsdp')
- moment_vec: float32 [11264], P('fsdp')
- second_vec: float32 [11264], P('fsdp')
Outputs:
- output 1: float32 [29491200], P('fsdp')
- output 2: float32 [29491200], P('fsdp')
- output 3: float32 [29491200], P('fsdp')
- output 4: float32 [11264], P('fsdp')
- output 5: float32 [11264], P('fsdp')
- output 6: float32 [11264], P('fsdp')
- output 7: bfloat16 [29491200], replicated
- output 8: bfloat16 [11264], replicated
All inputs are finite; a program needn't handle non-finite values.
Results may differ from a plain program's by a relative error of at most 0.001.
Values are sent between devices in bfloat16 or wider.
A program may use at most 1 GiB of HBM per device.

v0:
```python
import jax
import jax.numpy as jnp
from jax import lax
from jax.sharding import PartitionSpec as P

STEP = 4
LEARN_RATE = 1e-3
BETA_ONE = 0.9
BETA_TWO = 0.999
ADAM_EPS = 1e-8
DECAY = 0.01
NORM_EPS = 1e-6
FIX_ONE = 1.0 - BETA_ONE ** STEP
FIX_TWO = 1.0 - BETA_TWO ** STEP


def adam_update(grad_sum, clip_coef, master, moment, second, decay):
    clip_grad = clip_coef * grad_sum
    new_moment = BETA_ONE * moment + (1.0 - BETA_ONE) * clip_grad
    new_second = BETA_TWO * second + (1.0 - BETA_TWO) * clip_grad * clip_grad
    step_dir = (new_moment / FIX_ONE) / (jnp.sqrt(new_second / FIX_TWO) + ADAM_EPS)
    new_master = master - LEARN_RATE * (step_dir + decay * master)
    return new_master, new_moment, new_second


def total_share(grad_block, group):
    rows = grad_block.reshape(group, grad_block.shape[1] // group)
    received = lax.all_to_all(rows, 'fsdp', 0, 0, tiled=True)
    return jnp.sum(received, axis=0, dtype=jnp.float32)


def solution(mesh):
    group = mesh.shape['fsdp']

    def local_step(grad_mat, grad_vec, master_mat, moment_mat, second_mat, master_vec, moment_vec, second_vec):
        sum_mat = total_share(grad_mat, group)
        sum_vec = total_share(grad_vec, group)
        local_square = jnp.sum(sum_mat * sum_mat) + jnp.sum(sum_vec * sum_vec)
        total_norm = jnp.sqrt(lax.psum(local_square, 'fsdp'))
        clip_coef = jnp.minimum(1.0, 1.0 / (total_norm + NORM_EPS))
        new_mat = adam_update(sum_mat, clip_coef, master_mat, moment_mat, second_mat, DECAY)
        new_vec = adam_update(sum_vec, clip_coef, master_vec, moment_vec, second_vec, 0.0)
        weights_mat = lax.all_gather(new_mat[0].astype(jnp.bfloat16), 'fsdp', tiled=True)
        weights_vec = lax.all_gather(new_vec[0].astype(jnp.bfloat16), 'fsdp', tiled=True)
        return new_mat + new_vec + (weights_mat, weights_vec)

    row_spec = P('fsdp', None)
    flat_spec = P('fsdp')
    whole_spec = P()
    return jax.shard_map(local_step, mesh=mesh,
                         in_specs=(row_spec, row_spec) + (flat_spec,) * 6,
                         out_specs=(flat_spec,) * 6 + (whole_spec, whole_spec),
                         check_vma=False)
```

profile of v0, /device:TPU:0, one launch (start us, length us, event | category | flops | bytes accessed | tf_op | source)
XLA Modules:
  0.0 2005.8 jit_solution(12255923114096903876)
XLA Ops:
  7.2 0.5 broadcast.21
  7.7 1.6 reduce.4
  9.2 0.7 reshape.31
  9.9 4.3 all-to-all-start.1
  14.2 368.5 %reduce.3 = bf16[8,3686400]{1,0:T(8,128)(2,1)} reduce(bf16[8,1,3686400]{2,1,0:T(2,128)(2,1)} %bitcast, bf16[]{:T(256)} %broadcast.21), dimensions={1}, to_apply=%bitcast.reduce_sub_computation | reduce | bytes 117964800 | tf_op jit(solution)/shard_map/all_to_all | solution.py:28
  382.8 300.8 %reshape.29 = bf16[8,2,1843200]{2,1,0:T(2,128)(2,1)} reshape(bf16[8,3686400]{1,0:T(8,128)(2,1)} %reduce.3) | data formatting | bytes 117964800
  683.6 7.9 all-to-all-start
  691.5 0.0 all-gather.3.cloned.1.call-start
  691.6 0.1 reshape.32
  691.7 0.1 convert_reduce_fusion.1
  691.7 0.6 multiply_reduce_fusion.1
  692.3 635.8 %all-to-all-done = bf16[8,2,1843200]{2,1,0:T(2,128)(2,1)} async-done(((bf16[8,2,1843200]{2,1,0:T(2,128)(2,1)}), bf16[8,2,1843200]{2,1,0:T(2,128)(2,1)}, u32[]{:S(2)}, u32[]{:S(2)}) %all-to-all-start) | async-done | bytes 58982432 | tf_op jit(solution)/shard_map/all_to_all | solution.py:28
  1328.1 134.9 %reshape.30 = bf16[8,1,3686400]{2,1,0:T(2,128)(2,1)} reshape(bf16[8,2,1843200]{2,1,0:T(2,128)(2,1)} %all-to-all-done) | data formatting | bytes 117964800
  1463.0 161.8 %convert_reduce_fusion = f32[3686400]{0:T(1024)} fusion(bf16[8,1,3686400]{2,1,0:T(2,128)(2,1)} %reshape.30), kind=kLoop, calls=%fused_computation | loop fusion | flops 55296000 | bytes 73728000 | tf_op jit(solution)/shard_map/reduce_sum | solution.py:29
  1624.8 7.9 multiply_reduce_fusion
  1634.0 22.2 %psum.7 = f32[]{:T(128)} all-reduce(f32[]{:T(128)S(6)} %add.38), channel_id=1, replica_groups=mesh['fsdp'=8] {'fsdp'}, use_global_device_ids=true, to_apply=%region_4.0 | all-reduce | flops 1 | bytes 8 | tf_op jit(solution)/shard_map/psum | solution.py:39
  1657.0 38.4 %fusion.4 = (bf16[3686400]{0:T(1024)(128)(2,1)}, f32[3686400]{0:T(1024)}, f32[3686400]{0:T(1024)}, f32[3686400]{0:T(1024)}) fusion(f32[3686400]{0:T(1024)} %param.10, f32[3686400]{0:T(1024)} %convert_reduce_fusion, f32[]{:T(128)S(6)} %min.3, f32[3686400]{0:T(1024)} %param.11, f32[3686400]{0:T(1024)} %param.12), kind=kLoop, calls=%fused_computation.13 | loop fusion | flops 62668800 | bytes 110592000 | tf_op jit(solution)/shard_map/convert_element_type | solution.py:43
  1695.4 0.0 all-gather.3.cloned.1.call-update
  1695.5 0.6 fusion.2
  1696.1 12.0 all-gather
  1708.1 0.1 reduce.2
  1708.2 0.7 reshape.27
  1708.9 250.5 %all-gather.3.cloned.1.call-done = bf16[29491200]{0:T(1024)(128)(2,1)} async-done(((bf16[3686400]{0:T(1024)(128)(2,1)}), bf16[29491200]{0:T(1024)(128)(2,1)}) %all-gather.3.cloned.1.call-update) | async-done | bytes 58982416 | tf_op jit(solution)/shard_map/all_gather | solution.py:43
  1959.4 39.2 %copy.17 = bf16[29491200]{0:T(1024)(128)(2,1)} copy(bf16[29491200]{0:T(1024)(128)(2,1)} %all-gather.3.cloned.1.call-done) | data formatting | bytes 117964800
  (8 shorter events, 0.0 us)
Async XLA Ops:
  9.9 673.7 %all-to-all-start.1 = ((bf16[8,2,704]{2,1,0:T(2,128)(2,1)}), bf16[8,2,704]{2,1,0:T(2,128)(2,1)S(1)}, u32[]{:S(2)}, u32[]{:S(2)}) async-start(bf16[8,2,704]{2,1,0:T(2,128)(2,1)} %reshape.31), calls=%async_computation.1 | async-start | bytes 49152 | tf_op jit(solution)/shard_map/all_to_all | solution.py:28
  683.6 644.5 %all-to-all-start = ((bf16[8,2,1843200]{2,1,0:T(2,128)(2,1)}), bf16[8,2,1843200]{2,1,0:T(2,128)(2,1)}, u32[]{:S(2)}, u32[]{:S(2)}) async-start(bf16[8,2,1843200]{2,1,0:T(2,128)(2,1)} %reshape.29), calls=%async_computation | async-start | bytes 117964800 | tf_op jit(solution)/shard_map/all_to_all | solution.py:28
  691.5 1267.9 %all-gather.3.cloned.1.call-start = ((), (), s32[]{:S(2)}) async-start(), calls=%async_computation.2 | async-start | bytes 66355200 | tf_op jit(solution)/shard_map/all_gather | solution.py:43
  1657.0 38.4 %copy-start = (f32[1408]{0:T(1024)S(1)}, f32[1408]{0:T(1024)}, u32[]{:S(2)}) copy-start(f32[1408]{0:T(1024)} %param.13) | copy-start | bytes 16900
  1657.0 38.4 %copy-start.1 = (f32[1408]{0:T(1024)S(1)}, f32[1408]{0:T(1024)}, u32[]{:S(2)}) copy-start(f32[1408]{0:T(1024)} %param.14) | copy-start | bytes 16900
  1657.0 38.4 %copy-start.2 = (f32[1408]{0:T(1024)S(1)}, f32[1408]{0:T(1024)}, u32[]{:S(2)}) copy-start(f32[1408]{0:T(1024)} %param.15) | copy-start | bytes 16900
Sparse Core Ops, SparseCore 0:
  1695.6 263.7 all-gather.2
where the time goes:
time: 2020 us; the launch traced here: 2010 us
  waiting for transfers between devices  886 us (44%)
  other arithmetic  580 us (29%)
  local copies, waits for them, and re-layouts  477 us (24%)
  blocking collectives  34.2 us (2%)
    all_to_all x2, waiting for transfers between devices, total_share(): received = lax.all_to_all(rows, 'fsdp', 0, 0, tiled=True)  636 us
    unnamed x13, local copies, waits for them, and re-layouts  476 us
    all_to_all x2, other arithmetic, total_share(): received = lax.all_to_all(rows, 'fsdp', 0, 0, tiled=True)  370 us
    all_gather x1, waiting for transfers between devices, local_step(): lax.all_gather(new_mat[0].astype(jnp.bfloat16), 'fsdp', tiled=True)  250 us
    reduce_sum x2, other arithmetic, total_share(): return jnp.sum(received, axis=0, dtype=jnp.float32)  162 us
  transfers between devices with their start and end apart: 3, of which 2 were waited for; matrix products, arithmetic and copies ran while one was open for 33% of the time, Pallas kernels for 0%

commit v1 on v0

v1 whole, which is shorter than its diff:
```python
import functools

import jax
import jax.numpy as jnp
from jax import lax
from jax.experimental import pallas as pl
from jax.experimental.pallas import tpu as pltpu
from jax.sharding import PartitionSpec as P

STEP = 4
LEARN_RATE = 1e-3
BETA_ONE = 0.9
BETA_TWO = 0.999
ADAM_EPS = 1e-8
DECAY = 0.01
NORM_EPS = 1e-6
FIX_ONE = 1.0 - BETA_ONE ** STEP
FIX_TWO = 1.0 - BETA_TWO ** STEP

MESH = pl.DeviceIdType.MESH
LANES = 128
BLK = 80
CHUNKS = 20
ADAM_ROWS = 720
SPLITS = (5, 27, 8)
VMEM_MAX = 64 * 1024 * 1024 - 64 * 1024


def adam_update(grad_sum, clip_coef, master, moment, second, decay):
    clip_grad = clip_coef * grad_sum
    new_moment = BETA_ONE * moment + (1.0 - BETA_ONE) * clip_grad
    new_second = BETA_TWO * second + (1.0 - BETA_TWO) * clip_grad * clip_grad
    step_dir = (new_moment / FIX_ONE) / (jnp.sqrt(new_second / FIX_TWO) + ADAM_EPS)
    new_master = master - LEARN_RATE * (step_dir + decay * master)
    return new_master, new_moment, new_second


def remote(src, dst, send_sem, recv_sem, dev):
    return pltpu.make_async_remote_copy(src_ref=src, dst_ref=dst, send_sem=send_sem, recv_sem=recv_sem,
                                        device_id=(dev,), device_id_type=MESH)


def scatter_kernel(share, rows, chunks, graw, vraw, g_out, gv_out, c_out,
                   raw, send_p, send_x, send_y, own, recv_p, recv_x, recv_y, part_s, part_r, total,
                   vbuf, vsend, vall, nsend, nall, acc,
                   load_sem, out_sem, sp_sem, sx_sem, sy_sem, rp_sem, rx_sem, ry_sem, ps_sem, pr_sem,
                   free_sem, pfree_sem, vload_sem, vs_sem, vr_sem, ns_sem, nr_sem):
    me = lax.axis_index('fsdp')
    core, cx, cy = lax.rem(me, 2), lax.rem(me // 2, 2), me // 4
    mate, ox, oy = 1 - core, 1 - cx, 1 - cy

    def dev(y, x, c):
        return 4 * y + 2 * x + c

    half = share // 2
    width = rows * LANES

    barrier = pltpu.get_barrier_semaphore()
    for d in range(1, 8):
        pl.semaphore_signal(barrier, inc=1, device_id=(lax.rem(me + d, 8),), device_id_type=MESH)

    pieces = []
    for j in range(2):
        pieces += [(dev(cy, ox, j), 0), (dev(oy, ox, j), 0)]
    for j in range(2):
        pieces += [(dev(oy, cx, j), 1), (dev(oy, ox, j), 1)]
    for c in (mate, core):
        pieces += [(dev(cy, cx, c), 0), (dev(oy, cx, c), 0), (dev(cy, cx, c), 1), (dev(cy, ox, c), 1)]

    def start_load(t, slot):
        for q, (s, h) in enumerate(pieces):
            off = pl.multiple_of((s * share + h * half + t * rows) * LANES, 2048)
            pltpu.make_async_copy(graw.at[:, pl.ds(off, width)], raw.at[slot, :, pl.ds(q * width, width)],
                                  load_sem.at[slot]).start()

    def wait_load(slot):
        pltpu.make_async_copy(graw.at[:, pl.ds(0, 16 * width)], raw.at[slot], load_sem.at[slot]).wait()

    def squeeze(slot, q, dst, base):
        def body(i, carry):
            col = pl.multiple_of(q * width + i * (BLK * LANES), 2048)
            vals = raw[slot, :, pl.ds(col, BLK * LANES)].astype(jnp.float32).reshape(BLK, LANES)
            dst[pl.ds(pl.multiple_of(base + i * BLK, 16), BLK), :] = vals.astype(jnp.bfloat16)
            return carry
        lax.fori_loop(0, rows // BLK, body, 0)

    def copies(slot):
        out = []
        for j in range(2):
            out.append(remote(send_x.at[slot, j], recv_x.at[slot, core], sx_sem.at[slot, j], rx_sem.at[slot, core],
                              dev(cy, ox, j)))
            out.append(remote(send_y.at[slot, j], recv_y.at[slot, core], sy_sem.at[slot, j], ry_sem.at[slot, core],
                              dev(oy, cx, j)))
        out.append(remote(send_p.at[slot], recv_p.at[slot], sp_sem.at[slot], rp_sem.at[slot], dev(cy, cx, mate)))
        return out

    def wait_arrivals(slot):
        for j in range(2):
            remote(send_x.at[slot, j], recv_x.at[slot, j], sx_sem.at[slot, j], rx_sem.at[slot, j],
                   dev(cy, ox, j)).wait_recv()
            remote(send_y.at[slot, j], recv_y.at[slot, j], sy_sem.at[slot, j], ry_sem.at[slot, j],
                   dev(oy, cx, j)).wait_recv()
        remote(send_p.at[slot], recv_p.at[slot], sp_sem.at[slot], rp_sem.at[slot], dev(cy, cx, mate)).wait_recv()

    def part_copies(slot):
        return [remote(part_s.at[slot, 0], part_r.at[slot, 0], ps_sem.at[slot, 0], pr_sem.at[slot, 0],
                       dev(oy, cx, core)),
                remote(part_s.at[slot, 1], part_r.at[slot, 1], ps_sem.at[slot, 1], pr_sem.at[slot, 1],
                       dev(cy, ox, core))]

    def out_copies(t, slot):
        return [pltpu.make_async_copy(total.at[slot, h],
                                      g_out.at[pl.ds(pl.multiple_of(h * half + t * rows, 16), rows), :],
                                      out_sem.at[slot, h]) for h in range(2)]

    def give_credit():
        pl.semaphore_signal(free_sem.at[0], inc=1, device_id=(dev(cy, cx, mate),), device_id_type=MESH)
        for j in range(2):
            pl.semaphore_signal(free_sem.at[1 + core], inc=1, device_id=(dev(cy, ox, j),), device_id_type=MESH)
            pl.semaphore_signal(free_sem.at[3 + core], inc=1, device_id=(dev(oy, cx, j),), device_id_type=MESH)

    def four_sum(slot, h, k, dst):
        far = recv_x if h == 0 else recv_y
        q = 2 * h + k

        def body(i, carry):
            at = pl.ds(pl.multiple_of(q * rows + i * BLK, 16), BLK)
            fat = pl.ds(pl.multiple_of(k * rows + i * BLK, 16), BLK)
            vals = (own[slot, at, :].astype(jnp.float32) + recv_p[slot, at, :].astype(jnp.float32)
                    + far[slot, 0, fat, :].astype(jnp.float32) + far[slot, 1, fat, :].astype(jnp.float32))
            dst[slot, h, pl.ds(pl.multiple_of(i * BLK, 16), BLK), :] = vals
            return carry
        lax.fori_loop(0, rows // BLK, body, 0)

    start_load(0, 0)
    vload = pltpu.make_async_copy(vraw, vbuf, vload_sem)
    vload.start()
    acc[...] = jnp.zeros_like(acc)
    vload.wait()
    vec_bf = vbuf[...].astype(jnp.float32).reshape(vsend.shape).astype(jnp.bfloat16)
    vsend[...] = vec_bf
    vall[me] = vec_bf
    pl.semaphore_wait(barrier, 7)

    def vec_copy(d):
        return remote(vsend, vall.at[me], vs_sem.at[d], vr_sem.at[me], lax.rem(me + d, 8))

    for d in range(1, 8):
        vec_copy(d).start()

    def step(i, carry):
        slot, prev = lax.rem(i, 2), lax.rem(i + 1, 2)

        @pl.when(i + 1 < chunks)
        def _():
            start_load(i + 1, prev)

        @pl.when(i < chunks)
        def _():
            wait_load(slot)

            @pl.when(i >= 2)
            def _():
                for copy in copies(slot):
                    copy.wait_send()

            for j in range(2):
                for k in range(2):
                    squeeze(slot, 2 * j + k, send_x.at[slot, j], k * rows)
                    squeeze(slot, 4 + 2 * j + k, send_y.at[slot, j], k * rows)
            for q in range(4):
                squeeze(slot, 8 + q, send_p.at[slot], q * rows)
            for q in range(4):
                squeeze(slot, 12 + q, own.at[slot], q * rows)

            @pl.when(i >= 2)
            def _():
                for n in range(5):
                    pl.semaphore_wait(free_sem.at[n], 1)

            for copy in copies(slot):
                copy.start()

        @pl.when((i >= 1) & (i <= chunks))
        def _():
            wait_arrivals(prev)

            @pl.when(i >= 3)
            def _():
                for copy in part_copies(prev):
                    copy.wait_send()
                for n in range(2):
                    pl.semaphore_wait(pfree_sem.at[n], 1)
                for copy in out_copies(i - 3, prev):
                    copy.wait()

            four_sum(prev, 0, 1, part_s)
            four_sum(prev, 1, 1, part_s)
            four_sum(prev, 0, 0, total)
            four_sum(prev, 1, 0, total)
            for copy in part_copies(prev):
                copy.start()

            @pl.when(i - 1 < chunks - 2)
            def _():
                give_credit()

        @pl.when(i >= 2)
        def _():
            for copy in part_copies(slot):
                copy.wait_recv()
            for h in range(2):
                def body(n, run):
                    at = pl.ds(pl.multiple_of(n * BLK, 16), BLK)
                    vals = total[slot, h, at, :] + part_r[slot, h, at, :]
                    total[slot, h, at, :] = vals
                    return run + jnp.sum((vals * vals).reshape(BLK // 8, 8, LANES), axis=0)
                acc[...] += lax.fori_loop(0, rows // BLK, body, jnp.zeros((8, LANES), jnp.float32))
            for copy in out_copies(i - 2, slot):
                copy.start()

            @pl.when(i - 2 < chunks - 2)
            def _():
                pl.semaphore_signal(pfree_sem.at[0], inc=1, device_id=(dev(oy, cx, core),), device_id_type=MESH)
                pl.semaphore_signal(pfree_sem.at[1], inc=1, device_id=(dev(cy, ox, core),), device_id_type=MESH)
        return carry

    lax.fori_loop(0, chunks + 2, step, 0)

    nsend[...] = acc[...]
    nall[me] = acc[...]

    def norm_copy(d):
        return remote(nsend, nall.at[me], ns_sem.at[d], nr_sem.at[me], lax.rem(me + d, 8))

    for d in range(1, 8):
        j = lax.rem(me + d, 8)
        remote(vsend, vall.at[j], vs_sem.at[d], vr_sem.at[j], j).wait_recv()
    vec_sum = vall[0].astype(jnp.float32)
    for j in range(1, 8):
        vec_sum = vec_sum + vall[j].astype(jnp.float32)
    gv_out[...] = vec_sum
    square = jnp.sum((vec_sum * vec_sum).reshape(-1, 8, LANES), axis=0)
    for d in range(1, 8):
        norm_copy(d).start()
    for d in range(1, 8):
        j = lax.rem(me + d, 8)
        remote(nsend, nall.at[j], ns_sem.at[d], nr_sem.at[j], j).wait_recv()
    for j in range(8):
        square = square + nall[j]
    total_norm = jnp.sqrt(jnp.full((8, LANES), jnp.sum(square), jnp.float32))
    c_out[...] = jnp.minimum(1.0, 1.0 / (total_norm + NORM_EPS))

    for t in (chunks - 2, chunks - 1):
        for copy in copies(t % 2):
            copy.wait_send()
        for copy in part_copies(t % 2):
            copy.wait_send()
        for copy in out_copies(t, t % 2):
            copy.wait()
    for d in range(1, 8):
        vec_copy(d).wait_send()
        norm_copy(d).wait_send()


def reduce_grads(grad_mat, grad_vec):
    share = grad_mat.shape[1] // 8 // LANES
    vrows = grad_vec.shape[1] // LANES
    rows = share // 2 // CHUNKS
    bf, f32 = jnp.bfloat16, jnp.float32
    vm, dma = pltpu.VMEM, pltpu.SemaphoreType.DMA
    scratch = [
        vm((2, 1, 16 * rows * LANES), bf),
        vm((2, 4 * rows, LANES), bf), vm((2, 2, 2 * rows, LANES), bf), vm((2, 2, 2 * rows, LANES), bf),
        vm((2, 4 * rows, LANES), bf),
        vm((2, 4 * rows, LANES), bf), vm((2, 2, 2 * rows, LANES), bf), vm((2, 2, 2 * rows, LANES), bf),
        vm((2, 2, rows, LANES), f32), vm((2, 2, rows, LANES), f32), vm((2, 2, rows, LANES), f32),
        vm((1, vrows * LANES), bf), vm((vrows, LANES), bf), vm((8, vrows, LANES), bf),
        vm((8, LANES), f32), vm((8, 8, LANES), f32), vm((8, LANES), f32),
        dma((2,)), dma((2, 2)), dma((2,)), dma((2, 2)), dma((2, 2)), dma((2,)), dma((2, 2)), dma((2, 2)),
        dma((2, 2)), dma((2, 2)),
        pltpu.SemaphoreType.REGULAR((5,)), pltpu.SemaphoreType.REGULAR((2,)),
        dma, dma((8,)), dma((8,)), dma((8,)), dma((8,)),
    ]
    hbm = pl.BlockSpec(memory_space=pl.ANY)
    vmem = pl.BlockSpec(memory_space=pltpu.VMEM)
    return pl.pallas_call(
        functools.partial(scatter_kernel, share, rows, CHUNKS),
        out_shape=(jax.ShapeDtypeStruct((share, LANES), f32), jax.ShapeDtypeStruct((vrows, LANES), f32),
                   jax.ShapeDtypeStruct((8, LANES), f32)),
        in_specs=[hbm, hbm], out_specs=(hbm, vmem, vmem),
        scratch_shapes=scratch,
        compiler_params=pltpu.CompilerParams(collective_id=0, has_side_effects=True, vmem_limit_bytes=VMEM_MAX),
        name='reduce_grads',
    )(grad_mat, grad_vec)


def adam_kernel(c_ref, g_ref, p_ref, m_ref, v_ref, *refs):
    new_p, new_m, new_v, w_ref = refs[-4:]
    coef = c_ref[0:1, :]
    master, moment, second = adam_update(g_ref[...], coef, p_ref[...], m_ref[...], v_ref[...], DECAY)
    new_p[...] = master
    new_m[...] = moment
    new_v[...] = second
    w_ref[...] = master.astype(jnp.bfloat16)


def adam_part(first, count, coef, grads, master, moment, second, before):
    share = grads.shape[0]
    f32 = jnp.float32
    block = pl.BlockSpec((ADAM_ROWS, LANES), lambda i: (first + i, 0))
    extra = [] if before is None else list(before)
    elems = count * ADAM_ROWS * LANES
    return pl.pallas_call(
        adam_kernel,
        grid=(count,),
        out_shape=[jax.ShapeDtypeStruct((share, LANES), f32)] * 3
        + [jax.ShapeDtypeStruct((count * ADAM_ROWS, LANES), jnp.bfloat16)],
        in_specs=[pl.BlockSpec((8, LANES), lambda i: (0, 0))] + [block] * 4
        + [pl.BlockSpec(memory_space=pl.ANY)] * len(extra),
        out_specs=[block] * 3 + [pl.BlockSpec((ADAM_ROWS, LANES), lambda i: (i, 0))],
        input_output_aliases={5 + n: n for n in range(len(extra))},
        cost_estimate=pl.CostEstimate(flops=20 * elems, bytes_accessed=30 * elems, transcendentals=2 * elems),
        name='adam',
    )(coef, grads, master, moment, second, *extra)


def place_kernel(src_ref, *refs):
    refs[-1][...] = src_ref[...]


def place_part(first, count, share, part, before):
    blocks = share // ADAM_ROWS
    extra = [] if before is None else [before]
    elems = 8 * count * ADAM_ROWS * LANES
    return pl.pallas_call(
        place_kernel,
        grid=(8, count),
        out_shape=jax.ShapeDtypeStruct((8 * share, LANES), jnp.bfloat16),
        in_specs=[pl.BlockSpec((ADAM_ROWS, LANES), lambda d, i: (d * count + i, 0))]
        + [pl.BlockSpec(memory_space=pl.ANY)] * len(extra),
        out_specs=pl.BlockSpec((ADAM_ROWS, LANES), lambda d, i: (d * blocks + first + i, 0)),
        input_output_aliases={1 + n: n for n in range(len(extra))},
        cost_estimate=pl.CostEstimate(flops=elems, bytes_accessed=4 * elems, transcendentals=0),
        name='place',
    )(part, *extra)


def solution(mesh):
    def local_step(grad_mat, grad_vec, master_mat, moment_mat, second_mat, master_vec, moment_vec, second_vec):
        grads, vec_sum, coef = reduce_grads(grad_mat, grad_vec)
        share = grads.shape[0]
        state = [a.reshape(share, LANES) for a in (master_mat, moment_mat, second_mat)]
        first, new_mat, gathered = 0, None, []
        for count in SPLITS:
            *new_mat, part = adam_part(first, count, coef, grads, *state, new_mat)
            gathered.append(lax.all_gather(part.reshape(-1), 'fsdp', tiled=True))
            first += count
        first, weights = 0, None
        for count, part in zip(SPLITS, gathered):
            weights = place_part(first, count, share, part.reshape(-1, LANES), weights)
            first += count

        vshare = master_vec.shape[0]
        my_vec = lax.dynamic_slice(vec_sum.reshape(-1), (lax.axis_index('fsdp') * vshare,), (vshare,))
        new_vec = adam_update(my_vec, coef[0, 0], master_vec, moment_vec, second_vec, 0.0)
        weights_vec = lax.all_gather(new_vec[0].astype(jnp.bfloat16), 'fsdp', tiled=True)
        return tuple(a.reshape(-1) for a in new_mat) + new_vec + (weights.reshape(-1), weights_vec)

    row_spec = P('fsdp', None)
    flat_spec = P('fsdp')
    whole_spec = P()
    return jax.shard_map(local_step, mesh=mesh,
                         in_specs=(row_spec, row_spec) + (flat_spec,) * 6,
                         out_specs=(flat_spec,) * 6 + (whole_spec, whole_spec),
                         check_vma=False)
```

time: 2020 us -> 899 us (0.45)
  waiting for transfers between devices: 886 us -> 143 us
  Pallas kernels: 0 us -> 720 us
  other arithmetic: 580 us -> 2.18 us
  local copies, waits for them, and re-layouts: 477 us -> 1.88 us
  blocking collectives: 34.2 us -> 11.6 us
    pallas_call x0 -> x7, Pallas kernels: none -> 720 us  [the longest x1 488 us: reduce_grads(): pl.pallas_call(functools.partial(scatter_kernel, share, rows, CHUNKS), ou...]
    all_to_all x2 -> x0, waiting for transfers between devices: 636 us -> none  [total_share(): received = lax.all_to_all(rows, 'fsdp', 0, 0, tiled=True)]
    unnamed x13 -> x8, local copies, waits for them, and re-layouts: 476 us -> 0.69 us
    all_to_all x2 -> x0, other arithmetic: 370 us -> none  [total_share(): received = lax.all_to_all(rows, 'fsdp', 0, 0, tiled=True)]
    reduce_sum x4 -> x0, other arithmetic: 170 us -> none  [the longest x2 162 us: total_share(): return jnp.sum(received, axis=0, dtype=jnp.float32)]
    all_gather x1 -> x3, waiting for transfers between devices: 250 us -> 143 us  [local_step(): gathered.append(lax.all_gather(part.reshape(-1), 'fsdp', tiled=True))]
    convert_element_type x1 -> x0, other arithmetic: 38.4 us -> none  [local_step(): new_mat[0].astype(jnp.bfloat16)]
    psum x1 -> x0, blocking collectives: 22.2 us -> none  [local_step(): total_norm = jnp.sqrt(lax.psum(local_square, 'fsdp'))]
  transfers between devices with their start and end apart: 3 -> 3, of which waited for: 2 -> 1; matrix products, arithmetic and copies ran while one was open for 33% -> 0% of each run, Pallas kernels for 0% -> 21%
where the time goes in v1:
time: 899 us; the launch traced here: 893 us
  Pallas kernels  720 us (80%)
  waiting for transfers between devices  143 us (16%)
  between operations  13.8 us (2%)
  blocking collectives  11.6 us (1%)
    pallas_call x1, Pallas kernels, reduce_grads(): pl.pallas_call(functools.partial(scatter_kernel, share, rows, CHUNKS), ou...  488 us
    pallas_call x3, Pallas kernels, place_part(): pl.pallas_call(place_kernel, grid=(8, count), out_shape=jax.ShapeDtypeStr...  177 us
    all_gather x3, waiting for transfers between devices, local_step(): gathered.append(lax.all_gather(part.reshape(-1), 'fsdp', tiled=True))  143 us
    pallas_call x3, Pallas kernels, adam_part(): pl.pallas_call(adam_kernel, grid=(count,), out_shape=[jax.ShapeDtypeStruc...  55 us
  transfers between devices with their start and end apart: 3, of which 1 were waited for; matrix products, arithmetic and copies ran while one was open for 0% of the time, Pallas kernels for 21%

profile of v1, /device:TPU:0, one launch (start us, length us, event | category | flops | bytes accessed | tf_op | source)
XLA Modules:
  0.0 892.6 jit_solution(7533899293642561296)
XLA Ops:
  7.2 0.0 all-gather.9.cloned.1.call-start
  7.2 487.7 %reduce_grads.1 = (f32[28800,128]{1,0:T(8,128)}, f32[88,128]{1,0:T(8,128)}, f32[8,128]{1,0:T(8,128)}) custom-call(bf16[1,29491200]{1,0:T(2,128)(2,1)} %graw.1, bf16[1,11264]{1,0:T(2,128)(2,1)} %vraw.1), custom_call_target="tpu_custom_call" | custom-call | tf_op jit(solution)/shard_map/reduce_grads/pallas_call | solution.py:287
  495.0 7.9 adam.3
  502.8 0.0 all-gather.9.cloned.1.call-update
  502.8 0.0 all-gather.7.cloned.1.call-start
  502.9 36.2 %adam.4 = (f32[28800,128]{1,0:T(8,128)}, f32[28800,128]{1,0:T(8,128)}, f32[28800,128]{1,0:T(8,128)}, bf16[19440,128]{1,0:T(8,128)(2,1)}) custom-call(f32[8,128]{1,0:T(8,128)} %get-tuple-element.23.c_ref, f32[28800,128]{1,0:T(8,128)} %get-tuple-element.24.g_ref, f32[28800,128]{1,0:T(8,128)} %bitcast.17, ...), custom_call_target="tpu_custom_call", output_to_operand_aliasing={{0}: (5, {}), {1}: (6, {}), {2}: (7, {})} | custom-call | flops 49766400 | bytes 74649600 | tf_op jit(solution)/shard_map/adam/pallas_call | solution.py:314
  539.1 0.0 all-gather.7.cloned.1.call-update
  539.1 0.0 all-gather.5.cloned.1.call-start
  539.2 0.0 copy-start
  539.2 0.0 copy-start.1
  539.2 0.0 copy-start.2
  539.2 11.0 %adam.5 = (f32[28800,128]{1,0:T(8,128)}, f32[28800,128]{1,0:T(8,128)}, f32[28800,128]{1,0:T(8,128)}, bf16[5760,128]{1,0:T(8,128)(2,1)}) custom-call(f32[8,128]{1,0:T(8,128)} %get-tuple-element.23.c_ref, f32[28800,128]{1,0:T(8,128)} %get-tuple-element.24.g_ref, f32[28800,128]{1,0:T(8,128)} %bitcast.18, ...), custom_call_target="tpu_custom_call", output_to_operand_aliasing={{0}: (5, {}), {1}: (6, {}), {2}: (7, {})} | custom-call | flops 14745600 | bytes 22118400 | tf_op jit(solution)/shard_map/adam/pallas_call | solution.py:314
  550.2 0.0 all-gather.5.cloned.1.call-update
  550.2 1.2 slice.3
  551.4 0.0 copy-done
  551.4 0.0 copy-done.2
  551.4 2.1 fusion.1
  553.5 11.6 %all-gather = bf16[8,1,1408]{2,1,0:T(2,128)(2,1)S(1)} all-gather(bf16[1,1,1408]{2,1,0:T(2,128)(2,1)S(1)} %reshape.72), channel_id=1, replica_groups=mesh['fsdp'=8] {'fsdp'}, dimensions={0}, use_global_device_ids=true | all-gather | bytes 25344 | tf_op jit(solution)/shard_map/all_gather | solution.py:367
  565.1 0.1 reduce
  565.2 0.7 reshape.73
  565.9 22.8 %place.3.refs_0_ = bf16[230400,128]{1,0:T(8,128)(2,1)} custom-call(bf16[28800,128]{1,0:T(8,128)(2,1)} %bitcast.30), custom_call_target="tpu_custom_call" | custom-call | flops 3686400 | bytes 14745600 | tf_op jit(solution)/shard_map/place/pallas_call | solution.py:336
  588.6 143.4 %all-gather.7.cloned.1.call-done = bf16[19906560]{0:T(1024)(128)(2,1)} async-done(((bf16[2488320]{0:T(1024)(128)(2,1)}), bf16[19906560]{0:T(1024)(128)(2,1)}) %all-gather.7.cloned.1.call-update) | async-done | bytes 39813136 | tf_op jit(solution)/shard_map/all_gather | solution.py:357
  732.0 118.3 %place.4.refs_0_ = bf16[230400,128]{1,0:T(8,128)(2,1)} custom-call(bf16[155520,128]{1,0:T(8,128)(2,1)} %bitcast.28, bf16[230400,128]{1,0:T(8,128)(2,1)} %place.3.refs_0_), custom_call_target="tpu_custom_call", output_to_operand_aliasing={{}: (1, {})} | custom-call | flops 19906560 | bytes 79626240 | tf_op jit(solution)/shard_map/place/pallas_call | solution.py:336
  850.3 35.8 %place.5 = bf16[230400,128]{1,0:T(8,128)(2,1)} custom-call(bf16[46080,128]{1,0:T(8,128)(2,1)} %bitcast.29, bf16[230400,128]{1,0:T(8,128)(2,1)} %place.4.refs_0_), custom_call_target="tpu_custom_call", output_to_operand_aliasing={{}: (1, {})} | custom-call | flops 5898240 | bytes 23592960 | tf_op jit(solution)/shard_map/place/pallas_call | solution.py:336
  (4 shorter events, 0.0 us)
Async XLA Ops:
  7.2 558.7 %all-gather.9.cloned.1.call-start = ((), (), s32[]{:S(2)}) async-start(), calls=%async_computation.2 | async-start | bytes 8294400 | tf_op jit(solution)/shard_map/all_gather | solution.py:357
  502.8 229.2 %all-gather.7.cloned.1.call-start = ((), (), s32[]{:S(2)}) async-start(), calls=%async_computation.1 | async-start | bytes 44789760 | tf_op jit(solution)/shard_map/all_gather | solution.py:357
  539.1 311.2 %all-gather.5.cloned.1.call-start = ((), (), s32[]{:S(2)}) async-start(), calls=%async_computation | async-start | bytes 13271040 | tf_op jit(solution)/shard_map/all_gather | solution.py:357
  539.2 12.2 %copy-start = (f32[1408]{0:T(1024)S(1)}, f32[1408]{0:T(1024)}, u32[]{:S(2)}) copy-start(f32[1408]{0:T(1024)} %param.13) | copy-start | bytes 16900
  539.2 12.2 %copy-start.1 = (f32[1408]{0:T(1024)S(1)}, f32[1408]{0:T(1024)}, u32[]{:S(2)}) copy-start(f32[1408]{0:T(1024)} %param.14) | copy-start | bytes 16900
  539.2 12.2 %copy-start.2 = (f32[1408]{0:T(1024)S(1)}, f32[1408]{0:T(1024)}, u32[]{:S(2)}) copy-start(f32[1408]{0:T(1024)} %param.15) | copy-start | bytes 16900
Sparse Core Ops, SparseCore 0:
  503.0 44.3 all-gather.8
  549.2 182.7 all-gather.6
  733.8 62.9 all-gather.4
